TPU v7x, 32 devices: a whole 2x2x4 slice. The times are simulated.
32 devices in a mesh: ex: 8 (over y, x, core), tp: 4 (over z).
Axes of the slice: x: 2, y: 2, z: 4, core: 2. Of those that a mesh axis runs over, the one named last changes fastest.
Arguments:
- samples: bfloat16 [192, 2048], P(('ex', 'tp')), may hold values from -6 to 6
- gate_weight: bfloat16 [2048, 44], replicated, may hold values from -15 to 15
- up_weight: bfloat16 [16, 2048, 4096], P('ex', None, 'tp'), may hold values from -0.125 to 0.125
- down_weight: bfloat16 [16, 4096, 2048], P('ex', 'tp'), may hold values from -0.09375 to 0.09375
Outputs:
- task_outputs: bfloat16 [192, 5, 2048], P(('ex', 'tp'))
All inputs are finite; a program needn't handle non-finite values.
Results may differ from a plain program's by a relative error of at most 0.0055.
Values may be sent and summed in bfloat16 or wider, within the bound.
A program may use at most 128 MiB of HBM per device.

v0:
```python
import jax
import jax.numpy as jnp
import numpy as np
from jax import lax
from jax.sharding import PartitionSpec as P

TASKS = 4
TASK_EXP = 3
SHARED = 4
EXPERTS = 16
GATES = 44


def routing_table():
    per_task = TASK_EXP + SHARED
    table = np.zeros((GATES, (TASKS + 1) * EXPERTS), np.float32)
    for task_idx in range(TASKS):
        for column in range(per_task):
            if column < TASK_EXP:
                expert_idx = task_idx * TASK_EXP + column
            else:
                expert_idx = TASKS * TASK_EXP + column - TASK_EXP
            table[task_idx * per_task + column, task_idx * EXPERTS + expert_idx] = 1.0
    for expert_idx in range(EXPERTS):
        table[TASKS * per_task + expert_idx, TASKS * EXPERTS + expert_idx] = 1.0
    return jnp.asarray(table, dtype=jnp.float32)


def gate_mix(rows, gate_weight):
    logits = jnp.dot(rows, gate_weight, preferred_element_type=jnp.float32)
    per_task = TASK_EXP + SHARED
    pieces = []
    for task_idx in range(TASKS):
        pieces.append(
            jax.nn.softmax(logits[:, task_idx * per_task : (task_idx + 1) * per_task], axis=-1)
        )
    pieces.append(jax.nn.softmax(logits[:, TASKS * per_task :], axis=-1))
    probs = jnp.concatenate(pieces, axis=1)
    mixed = jnp.dot(probs, routing_table(), precision=lax.Precision.HIGHEST)
    return mixed.reshape(rows.shape[0], TASKS + 1, EXPERTS)


def on_device(samples, gate_weight, up_weight, down_weight):
    local_experts = up_weight.shape[0]
    ex_count = lax.axis_size("ex")
    tp_count = lax.axis_size("tp")
    row_dev = samples.shape[0]
    width = samples.shape[1]
    piece = lax.all_gather(samples, ("ex", "tp"), axis=0, tiled=True)
    outputs = []
    for expert_idx in range(local_experts):
        outputs.append(
            jnp.maximum(
                jnp.dot(piece, up_weight[expert_idx], preferred_element_type=jnp.float32), 0.0
            ).astype(jnp.bfloat16)
        )
    hidden = jnp.stack(outputs, axis=1)
    partial_out = jnp.einsum(
        "rlf,lfd->rld", hidden, down_weight, preferred_element_type=jnp.float32
    )
    blocked = partial_out.reshape(ex_count, tp_count * row_dev, local_experts, width)
    summed = lax.psum_scatter(blocked, "tp", scatter_dimension=1, tiled=True)
    gathered = lax.all_to_all(summed, "ex", split_axis=0, concat_axis=2, tiled=True)[0]
    mixing = gate_mix(samples, gate_weight)
    result = jnp.einsum("rke,red->rkd", mixing, gathered, precision=lax.Precision.HIGHEST)
    return result.astype(jnp.bfloat16)


def solution(mesh):
    placed = (P(("ex", "tp"), None), P(), P("ex", None, "tp"), P("ex", "tp", None))
    return jax.shard_map(
        on_device,
        mesh=mesh,
        in_specs=placed,
        out_specs=P(("ex", "tp"), None, None),
        check_vma=False,
    )
```

profile of v0, /device:TPU:0, one launch (start us, length us, event | category | flops | bytes accessed | tf_op | source)
XLA Modules:
  0.0 185.9 jit_solution(10094937951658092538)
XLA Ops:
  6.5 0.0 copy-start
  6.5 0.0 reduce-scatter.2.cloned.1.call-start
  6.5 78.9 %all-gather = bf16[32,6,2048]{2,1,0:T(8,128)(2,1)S(1)} all-gather(bf16[1,6,2048]{2,1,0:T(8,128)(2,1)} %bitcast.43), channel_id=1, replica_groups=mesh['ex'=8,'tp'=4] {'ex','tp'}, dimensions={0}, use_global_device_ids=true | all-gather | bytes 811008 | tf_op jit(solution)/shard_map/all_gather | solution.py:49
  85.5 0.3 reshape.20
  85.7 3.2 %fusion.21 = bf16[192,1,1024]{2,0,1:T(8,128)(2,1)S(1)} fusion(bf16[192,2048]{1,0:T(8,128)(2,1)S(1)} %reshape.20, bf16[2,2048,1024]{2,1,0:T(8,128)(2,1)} %param.7), kind=kOutput, calls=%fused_computation.12 | convolution fusion | flops 805699584 | bytes 5373952 | tf_op jit(solution)/shard_map/dot_general | solution.py:54
  88.9 3.2 %fusion.18 = bf16[192,1,1024]{2,0,1:T(8,128)(2,1)S(1)} fusion(bf16[192,2048]{1,0:T(8,128)(2,1)S(1)} %reshape.20, bf16[2,2048,1024]{2,1,0:T(8,128)(2,1)} %param.7), kind=kOutput, calls=%fused_computation.11 | convolution fusion | flops 805699584 | bytes 5373952 | tf_op jit(solution)/shard_map/dot_general | solution.py:54
  92.1 5.2 %fusion.24 = f32[2,192,2048]{2,1,0:T(8,128)S(1)} fusion(bf16[2,1024,2048]{2,1,0:T(8,128)(2,1)} %param.8, bf16[192,1,1024]{2,0,1:T(8,128)(2,1)S(1)} %fusion.21, bf16[192,1,1024]{2,0,1:T(8,128)(2,1)S(1)} %fusion.18), kind=kOutput, calls=%fused_computation.17 | convolution fusion | flops 1611005952 | bytes 12320768 | tf_op jit(solution)/shard_map/rlf,lfd->rld/dot_general | solution.py:58
  97.3 0.0 copy-start.1
  97.3 0.0 copy-start.5
  97.3 0.0 copy-start.6
  97.3 0.0 copy-start.4
  97.3 0.0 copy-start.3
  97.3 0.0 copy-start.2
  97.4 3.5 %copy.10 = f32[8,24,2,2048]{3,0,2,1:T(8,128)} copy(f32[8,24,2,2048]{3,1,0,2:T(8,128)S(1)} %bitcast.41) | data formatting | bytes 6291456 | tf_op jit(solution)/shard_map/reshape | solution.py:61
  100.8 0.0 reduce-scatter.2.cloned.1.call-update
  100.9 0.0 copy-done
  100.9 0.0 copy-done.1
  100.9 0.2 fusion.50
  101.0 0.2 slice_reduce_fusion
  101.2 0.2 slice_reduce_fusion.1
  101.5 0.2 fusion.37
  101.7 0.0 copy-done.5
  101.7 0.2 fusion.31
  101.9 0.0 copy-done.6
  101.9 0.2 convolution_add_fusion.3
  102.1 56.2 %reduce-scatter.2.cloned.1.call-done = f32[8,6,2,2048]{3,0,2,1:T(8,128)} async-done(((f32[8,24,2,2048]{3,0,2,1:T(8,128)}), f32[8,6,2,2048]{3,0,2,1:T(8,128)}) %reduce-scatter.2.cloned.1.call-update) | async-done | bytes 786448 | tf_op jit(solution)/shard_map/reduce_scatter | solution.py:62
  158.3 2.6 %copy.11 = f32[8,6,2,2048]{3,2,1,0:T(2,128)} copy(f32[8,6,2,2048]{3,0,2,1:T(8,128)} %reduce-scatter.2.cloned.1.call-done) | data formatting | bytes 1572864 | tf_op jit(solution)/shard_map/reduce_scatter | solution.py:62
  161.0 3.6 %all-to-all-start = ((f32[8,6,2,2048]{3,2,1,0:T(2,128)}), f32[8,6,2,2048]{3,2,1,0:T(2,128)S(1)}, u32[]{:S(2)}, u32[]{:S(2)}) async-start(f32[8,6,2,2048]{3,2,1,0:T(2,128)} %copy.11), calls=%async_computation.1 | async-start | bytes 1572864 | tf_op jit(solution)/shard_map/all_to_all | solution.py:63
  164.6 0.2 fusion.38
  164.8 0.0 copy-done.4
  164.8 0.2 convolution_add_fusion.2
  165.0 0.0 copy-done.3
  165.0 0.2 convolution_add_fusion.1
  165.2 0.0 copy-done.2
  165.2 0.2 convolution_add_fusion
  165.4 0.1 reshape.17
  165.5 11.7 %all-to-all-done = f32[8,6,2,2048]{3,2,1,0:T(2,128)S(1)} async-done(((f32[8,6,2,2048]{3,2,1,0:T(2,128)}), f32[8,6,2,2048]{3,2,1,0:T(2,128)S(1)}, u32[]{:S(2)}, u32[]{:S(2)}) %all-to-all-start) | async-done | bytes 786464 | tf_op jit(solution)/shard_map/all_to_all | solution.py:63
  177.2 0.1 copy.12
  177.2 0.5 squeeze.11
  177.8 0.5 convolution_convert_fusion
  178.3 0.8 copy.13
Async XLA Ops:
  6.5 94.3 %copy-start = (bf16[2048,44]{0,1:T(8,128)(2,1)S(1)}, bf16[2048,44]{0,1:T(8,128)(2,1)}, u32[]{:S(2)}) copy-start(bf16[2048,44]{0,1:T(8,128)(2,1)} %param.6) | copy-start | bytes 540676
  6.5 151.8 %reduce-scatter.2.cloned.1.call-start = ((), (), s32[]{:S(2)}) async-start(), calls=%async_computation.2 | async-start | bytes 3932160 | tf_op jit(solution)/shard_map/reduce_scatter | solution.py:62
  97.3 3.6 %copy-start.1 = (bf16[6,2048]{1,0:T(8,128)(2,1)S(1)}, bf16[6,2048]{1,0:T(8,128)(2,1)}, u32[]{:S(2)}) copy-start(bf16[6,2048]{1,0:T(8,128)(2,1)} %param.5) | copy-start | bytes 73732
  97.3 4.4 %copy-start.5 = (f32[7,80]{1,0:T(8,128)S(1)}, f32[7,80]{1,0:T(8,128)}, u32[]{:S(2)}) copy-start(f32[7,80]{1,0:T(8,128)} %constant.12) | copy-start | bytes 6724
  97.3 4.6 %copy-start.6 = (f32[7,80]{1,0:T(8,128)S(1)}, f32[7,80]{1,0:T(8,128)}, u32[]{:S(2)}) copy-start(f32[7,80]{1,0:T(8,128)} %constant.13) | copy-start | bytes 6724
  97.3 67.5 %copy-start.4 = (f32[7,80]{1,0:T(8,128)S(1)}, f32[7,80]{1,0:T(8,128)}, u32[]{:S(2)}) copy-start(f32[7,80]{1,0:T(8,128)} %constant.14) | copy-start | bytes 6724
  97.3 67.7 %copy-start.3 = (f32[7,80]{1,0:T(8,128)S(1)}, f32[7,80]{1,0:T(8,128)}, u32[]{:S(2)}) copy-start(f32[7,80]{1,0:T(8,128)} %constant.15) | copy-start | bytes 6724
  97.3 67.9 %copy-start.2 = (f32[16,80]{1,0:T(8,128)S(1)}, f32[16,80]{1,0:T(8,128)}, u32[]{:S(2)}) copy-start(f32[16,80]{1,0:T(8,128)} %constant.16) | copy-start | bytes 15364
  161.0 16.2 %all-to-all-start = ((f32[8,6,2,2048]{3,2,1,0:T(2,128)}), f32[8,6,2,2048]{3,2,1,0:T(2,128)S(1)}, u32[]{:S(2)}, u32[]{:S(2)}) async-start(f32[8,6,2,2048]{3,2,1,0:T(2,128)} %copy.11), calls=%async_computation.1 | async-start | bytes 1572864 | tf_op jit(solution)/shard_map/all_to_all | solution.py:63
Sparse Core Ops, SparseCore 0:
  101.0 57.3 reduce-scatter.1
where the time goes:
time: 186 us
  blocking collectives  78.9 us (42%)
  waiting for transfers between devices  67.9 us (37%)
  between operations  13.5 us (7%)
  matrix products  13.2 us (7%)
  local copies, waits for them, and re-layouts  7.84 us (4%)
  starting transfers between devices  3.65 us (2%)
    all_gather x1, blocking collectives, on_device(): piece = lax.all_gather(samples, ('ex', 'tp'), axis=0, tiled=True)  78.9 us
    reduce_scatter x1, waiting for transfers between devices, on_device(): summed = lax.psum_scatter(blocked, 'tp', scatter_dimension=1, tiled=True)  56.2 us
    all_to_all x1, waiting for transfers between devices, on_device(): lax.all_to_all(summed, 'ex', split_axis=0, concat_axis=2, tiled=True)[0]  11.7 us
    dot_general x2, matrix products, on_device(): jnp.dot(piece, up_weight[expert_idx], preferred_element_type=jnp.float32)  6.35 us
    dot_general x1, matrix products, on_device(): jnp.einsum('rlf,lfd->rld', hidden, down_weight, preferred_element_type=jn...  5.18 us
  transfers between devices with their start and end apart: 2, of which 2 were waited for; matrix products, arithmetic and copies ran while one was open for 1% of the time, Pallas kernels for 0%

commit v1 on v0

--- a/solution.py
+++ b/solution.py
@@ -46,7 +46,26 @@
     tp_count = lax.axis_size("tp")
     row_dev = samples.shape[0]
     width = samples.shape[1]
-    piece = lax.all_gather(samples, ("ex", "tp"), axis=0, tiled=True)
+    m_next, g_now, view_out = (
+        lax.axis_size(("ex", "tp")),
+        lax.axis_index(("ex", "tp")),
+        samples.shape[0],
+    )
+    spare, parts_out = (samples, 1)
+    while parts_out < m_next:
+        spare = jnp.concatenate(
+            [
+                spare,
+                lax.ppermute(
+                    spare,
+                    axis_name=("ex", "tp"),
+                    perm=tuple(((at, (at - parts_out) % m_next) for at in range(m_next))),
+                ),
+            ],
+            axis=0,
+        )
+        parts_out = 2 * parts_out
+    piece = jnp.roll(spare, g_now * view_out, axis=0)
     outputs = []
     for expert_idx in range(local_experts):
         outputs.append(

time: 186 us -> 154 us (0.83)
  blocking collectives: 78.9 us -> 0 us
  waiting for transfers between devices: 67.9 us -> 100 us
  starting transfers between devices: 3.65 us -> 11.7 us
  local copies, waits for them, and re-layouts: 7.84 us -> 11.3 us
  other arithmetic: 0.83 us -> 3.23 us
    all_gather x1 -> x0, blocking collectives: 78.9 us -> none  [on_device(): piece = lax.all_gather(samples, ('ex', 'tp'), axis=0, tiled=True)]
    ppermute x0 -> x5, waiting for transfers between devices: none -> 27.1 us  [on_device(): lax.ppermute(spare, axis_name=('ex', 'tp'), perm=tuple(((at, (at - parts_...]
    ppermute x0 -> x5, starting transfers between devices: none -> 8.04 us  [on_device(): lax.ppermute(spare, axis_name=('ex', 'tp'), perm=tuple(((at, (at - parts_...]
    reduce_scatter x1, waiting for transfers between devices: 56.2 us -> 61.5 us  [on_device(): summed = lax.psum_scatter(blocked, 'tp', scatter_dimension=1, tiled=True)]
    concatenate x0 -> x2, local copies, waits for them, and re-layouts: none -> 3.73 us  [the longest x1 2.57 us: on_device(): piece = jnp.roll(spare, g_now * view_out, axis=0)]
    concatenate x0 -> x3, other arithmetic: none -> 2.4 us  [on_device(): jnp.concatenate([spare, lax.ppermute(spare, axis_name=('ex', 'tp'), perm=...]
  transfers between devices with their start and end apart: 2 -> 7, of which waited for: 2 -> 7; matrix products, arithmetic and copies ran while one was open for 1% -> 1% of each run, Pallas kernels for 0% -> 0%
where the time goes in v1:
time: 154 us; the launch traced here: 153 us
  waiting for transfers between devices  100 us (65%)
  between operations  13.5 us (9%)
  matrix products  13.2 us (9%)
  starting transfers between devices  11.7 us (8%)
  local copies, waits for them, and re-layouts  11.3 us (7%)
  other arithmetic  3.23 us (2%)
    reduce_scatter x1, waiting for transfers between devices, on_device(): summed = lax.psum_scatter(blocked, 'tp', scatter_dimension=1, tiled=True)  61.5 us
    ppermute x5, waiting for transfers between devices, on_device(): lax.ppermute(spare, axis_name=('ex', 'tp'), perm=tuple(((at, (at - parts_...  27.1 us
    all_to_all x1, waiting for transfers between devices, on_device(): lax.all_to_all(summed, 'ex', split_axis=0, concat_axis=2, tiled=True)[0]  11.7 us
    ppermute x5, starting transfers between devices, on_device(): lax.ppermute(spare, axis_name=('ex', 'tp'), perm=tuple(((at, (at - parts_...  8.04 us
    dot_general x2, matrix products, on_device(): jnp.dot(piece, up_weight[expert_idx], preferred_element_type=jnp.float32)  6.36 us
    dot_general x1, matrix products, on_device(): jnp.einsum('rlf,lfd->rld', hidden, down_weight, preferred_element_type=jn...  5.18 us
    all_to_all x1, starting transfers between devices, on_device(): lax.all_to_all(summed, 'ex', split_axis=0, concat_axis=2, tiled=True)[0]  3.66 us
    reshape x1, local copies, waits for them, and re-layouts, on_device(): partial_out.reshape(ex_count, tp_count * row_dev, local_experts, width)  3.49 us
  transfers between devices with their start and end apart: 7, of which 7 were waited for; matrix products, arithmetic and copies ran while one was open for 1% of the time, Pallas kernels for 0%

profile of v1, /device:TPU:0, one launch (start us, length us, event | category | flops | bytes accessed | tf_op | source)
XLA Modules:
  0.0 153.3 jit_solution(12092282936366268955)
XLA Ops:
  6.5 0.0 copy-start
  6.5 0.0 reduce-scatter.2.cloned.1.call-start
  6.5 6.4 %collective-permute-start = (bf16[6,2048]{1,0:T(8,128)(2,1)}, bf16[6,2048]{1,0:T(8,128)(2,1)S(1)}, u32[]{:S(2)}, u32[]{:S(2)}) collective-permute-start(bf16[6,2048]{1,0:T(8,128)(2,1)} %param.5), channel_id=1, source_target_pairs={{0,31},{1,0},{2,1},{3,2},{4,3},{5,4},{6,5},{7,6},{8,7},{9,8},{10,9... | collective-permute-start | bytes 73736 | tf_op jit(solution)/shard_map/ppermute | solution.py:59
  12.9 1.9 %collective-permute-done = bf16[6,2048]{1,0:T(8,128)(2,1)S(1)} collective-permute-done((bf16[6,2048]{1,0:T(8,128)(2,1)}, bf16[6,2048]{1,0:T(8,128)(2,1)S(1)}, u32[]{:S(2)}, u32[]{:S(2)}) %collective-permute-start) | collective-permute-done | bytes 24608 | tf_op jit(solution)/shard_map/ppermute | solution.py:59
  14.9 0.8 pad_maximum_fusion.2
  15.6 0.1 collective-permute-start.1
  15.7 5.7 %collective-permute-done.1 = bf16[12,2048]{1,0:T(8,128)(2,1)S(1)} collective-permute-done((bf16[12,2048]{1,0:T(8,128)(2,1)S(1)}, bf16[12,2048]{1,0:T(8,128)(2,1)S(1)}, u32[]{:S(2)}, u32[]{:S(2)}) %collective-permute-start.1) | collective-permute-done | bytes 49184 | tf_op jit(solution)/shard_map/ppermute | solution.py:59
  21.5 0.8 pad_maximum_fusion.1
  22.3 0.1 collective-permute-start.2
  22.3 2.2 %collective-permute-done.2 = bf16[24,2048]{1,0:T(8,128)(2,1)S(1)} collective-permute-done((bf16[24,2048]{1,0:T(8,128)(2,1)S(1)}, bf16[24,2048]{1,0:T(8,128)(2,1)S(1)}, u32[]{:S(2)}, u32[]{:S(2)}) %collective-permute-start.2) | collective-permute-done | bytes 98336 | tf_op jit(solution)/shard_map/ppermute | solution.py:59
  24.5 0.8 pad_maximum_fusion
  25.4 0.2 collective-permute-start.3
  25.5 7.4 %collective-permute-done.3 = bf16[48,2048]{1,0:T(8,128)(2,1)S(1)} collective-permute-done((bf16[48,2048]{1,0:T(8,128)(2,1)S(1)}, bf16[48,2048]{1,0:T(8,128)(2,1)S(1)}, u32[]{:S(2)}, u32[]{:S(2)}) %collective-permute-start.3) | collective-permute-done | bytes 196640 | tf_op jit(solution)/shard_map/ppermute | solution.py:59
  32.9 1.2 concatenate.29
  34.1 1.3 collective-permute-start.4
  35.4 9.9 %collective-permute-done.4 = bf16[96,2048]{1,0:T(8,128)(2,1)S(1)} collective-permute-done((bf16[96,2048]{1,0:T(8,128)(2,1)S(1)}, bf16[96,2048]{1,0:T(8,128)(2,1)S(1)}, u32[]{:S(2)}, u32[]{:S(2)}) %collective-permute-start.4) | collective-permute-done | bytes 393248 | tf_op jit(solution)/shard_map/ppermute | solution.py:59
  45.3 2.6 %concatenate.30 = bf16[384,2048]{1,0:T(8,128)(2,1)S(1)} concatenate(bf16[6,2048]{1,0:T(8,128)(2,1)} %param.5, bf16[6,2048]{1,0:T(8,128)(2,1)S(1)} %collective-permute-done, bf16[12,2048]{1,0:T(8,128)(2,1)S(1)} %collective-permute-done.1, bf16[24,2048]{1,0:T(8,128)(2,1)S(1)} %collective-permute-done.2, bf16[48,2048]{1,0:T(8,128)(2,1)S(1)} %collective-permute-done.3, ...), dimensions={0} | concatenate | bytes 3145728 | tf_op jit(solution)/shard_map/jit(_roll_dynamic)/concatenate | solution.py:68
  47.9 3.2 %fusion.18 = bf16[192,1,1024]{2,0,1:T(8,128)(2,1)S(1)} fusion(bf16[2,2048,1024]{2,1,0:T(8,128)(2,1)} %param.7, bf16[384,2048]{1,0:T(8,128)(2,1)S(1)} %concatenate.30, s32[]{:T(128)S(6)} %select_n.14), kind=kOutput, calls=%fused_computation.11 | convolution fusion | flops 805699584 | bytes 5373956 | tf_op jit(solution)/shard_map/dot_general | solution.py:73
  51.0 3.2 %fusion.21 = bf16[192,1,1024]{2,0,1:T(8,128)(2,1)S(1)} fusion(bf16[2,2048,1024]{2,1,0:T(8,128)(2,1)} %param.7, bf16[384,2048]{1,0:T(8,128)(2,1)S(1)} %concatenate.30, s32[]{:T(128)S(6)} %select_n.14), kind=kOutput, calls=%fused_computation.12 | convolution fusion | flops 805699584 | bytes 5373956 | tf_op jit(solution)/shard_map/dot_general | solution.py:73
  54.2 5.2 %fusion.24 = f32[2,192,2048]{2,1,0:T(8,128)S(1)} fusion(bf16[2,1024,2048]{2,1,0:T(8,128)(2,1)} %param.8, bf16[192,1,1024]{2,0,1:T(8,128)(2,1)S(1)} %fusion.21, bf16[192,1,1024]{2,0,1:T(8,128)(2,1)S(1)} %fusion.18), kind=kOutput, calls=%fused_computation.17 | convolution fusion | flops 1611005952 | bytes 12320768 | tf_op jit(solution)/shard_map/rlf,lfd->rld/dot_general | solution.py:77
  59.4 0.0 copy-start.1
  59.4 0.0 copy-start.6
  59.4 0.0 copy-start.5
  59.5 3.5 %copy.10 = f32[8,24,2,2048]{3,0,2,1:T(8,128)} copy(f32[8,24,2,2048]{3,1,0,2:T(8,128)S(1)} %bitcast.38) | data formatting | bytes 6291456 | tf_op jit(solution)/shard_map/reshape | solution.py:80
  63.0 0.0 reduce-scatter.2.cloned.1.call-update
  63.0 0.0 copy-done
  63.0 0.2 fusion.54
  63.2 0.2 slice_reduce_fusion
  63.4 0.2 slice_reduce_fusion.1
  63.6 0.2 fusion.39
  63.8 0.2 fusion.33
  64.0 0.0 copy-done.5
  64.0 0.2 convolution_add_fusion.3
  64.2 61.5 %reduce-scatter.2.cloned.1.call-done = f32[8,6,2,2048]{3,0,2,1:T(8,128)} async-done(((f32[8,24,2,2048]{3,0,2,1:T(8,128)}), f32[8,6,2,2048]{3,0,2,1:T(8,128)}) %reduce-scatter.2.cloned.1.call-update) | async-done | bytes 786448 | tf_op jit(solution)/shard_map/reduce_scatter | solution.py:81
  125.7 2.6 %copy.11 = f32[8,6,2,2048]{3,2,1,0:T(2,128)} copy(f32[8,6,2,2048]{3,0,2,1:T(8,128)} %reduce-scatter.2.cloned.1.call-done) | data formatting | bytes 1572864 | tf_op jit(solution)/shard_map/reduce_scatter | solution.py:81
  128.3 3.7 %all-to-all-start = ((f32[8,6,2,2048]{3,2,1,0:T(2,128)}), f32[8,6,2,2048]{3,2,1,0:T(2,128)S(1)}, u32[]{:S(2)}, u32[]{:S(2)}) async-start(f32[8,6,2,2048]{3,2,1,0:T(2,128)} %copy.11), calls=%async_computation.1 | async-start | bytes 1572864 | tf_op jit(solution)/shard_map/all_to_all | solution.py:82
  132.0 0.2 fusion.40
  132.2 0.2 convolution_add_fusion.2
  132.4 0.0 copy-done.3
  132.4 0.2 convolution_add_fusion.1
  132.6 0.0 copy-done.2
  132.6 0.2 convolution_add_fusion
  132.8 0.1 reshape.17
  132.9 11.7 %all-to-all-done = f32[8,6,2,2048]{3,2,1,0:T(2,128)S(1)} async-done(((f32[8,6,2,2048]{3,2,1,0:T(2,128)}), f32[8,6,2,2048]{3,2,1,0:T(2,128)S(1)}, u32[]{:S(2)}, u32[]{:S(2)}) %all-to-all-start) | async-done | bytes 786464 | tf_op jit(solution)/shard_map/all_to_all | solution.py:82
  144.5 0.1 copy.12
  144.6 0.5 squeeze.11
  145.1 0.5 convolution_convert_fusion
  145.7 0.8 copy.13
  (6 shorter events, 0.0 us)
Async XLA Ops:
  6.5 56.4 %copy-start = (bf16[2048,44]{0,1:T(8,128)(2,1)S(1)}, bf16[2048,44]{0,1:T(8,128)(2,1)}, u32[]{:S(2)}) copy-start(bf16[2048,44]{0,1:T(8,128)(2,1)} %param.6) | copy-start | bytes 540676
  6.5 119.2 %reduce-scatter.2.cloned.1.call-start = ((), (), s32[]{:S(2)}) async-start(), calls=%async_computation.2 | async-start | bytes 3932160 | tf_op jit(solution)/shard_map/reduce_scatter | solution.py:81
  6.5 8.3 %collective-permute-start = (bf16[6,2048]{1,0:T(8,128)(2,1)}, bf16[6,2048]{1,0:T(8,128)(2,1)S(1)}, u32[]{:S(2)}, u32[]{:S(2)}) collective-permute-start(bf16[6,2048]{1,0:T(8,128)(2,1)} %param.5), channel_id=1, source_target_pairs={{0,31},{1,0},{2,1},{3,2},{4,3},{5,4},{6,5},{7,6},{8,7},{9,8},{10,9... | collective-permute-start | bytes 73736 | tf_op jit(solution)/shard_map/ppermute | solution.py:59
  15.6 5.8 %collective-permute-start.1 = (bf16[12,2048]{1,0:T(8,128)(2,1)S(1)}, bf16[12,2048]{1,0:T(8,128)(2,1)S(1)}, u32[]{:S(2)}, u32[]{:S(2)}) collective-permute-start(bf16[12,2048]{1,0:T(8,128)(2,1)S(1)} %pad_maximum_fusion.2), channel_id=1, source_target_pairs={{0,30},{1,31},{2,0},{3,1},{4,2},{5,3},{6,4},{7,5},{8,6},{9,7},{10,... | collective-permute-start | bytes 147464 | tf_op jit(solution)/shard_map/ppermute | solution.py:59
  22.3 2.3 %collective-permute-start.2 = (bf16[24,2048]{1,0:T(8,128)(2,1)S(1)}, bf16[24,2048]{1,0:T(8,128)(2,1)S(1)}, u32[]{:S(2)}, u32[]{:S(2)}) collective-permute-start(bf16[24,2048]{1,0:T(8,128)(2,1)S(1)} %pad_maximum_fusion.1), channel_id=1, source_target_pairs={{0,28},{1,29},{2,30},{3,31},{4,0},{5,1},{6,2},{7,3},{8,4},{9,5},{1... | collective-permute-start | bytes 294920 | tf_op jit(solution)/shard_map/ppermute | solution.py:59
  25.4 7.6 %collective-permute-start.3 = (bf16[48,2048]{1,0:T(8,128)(2,1)S(1)}, bf16[48,2048]{1,0:T(8,128)(2,1)S(1)}, u32[]{:S(2)}, u32[]{:S(2)}) collective-permute-start(bf16[48,2048]{1,0:T(8,128)(2,1)S(1)} %pad_maximum_fusion), channel_id=1, source_target_pairs={{0,24},{1,25},{2,26},{3,27},{4,28},{5,29},{6,30},{7,31},{8,0},{9,1... | collective-permute-start | bytes 589832 | tf_op jit(solution)/shard_map/ppermute | solution.py:59
  34.1 11.2 %collective-permute-start.4 = (bf16[96,2048]{1,0:T(8,128)(2,1)S(1)}, bf16[96,2048]{1,0:T(8,128)(2,1)S(1)}, u32[]{:S(2)}, u32[]{:S(2)}) collective-permute-start(bf16[96,2048]{1,0:T(8,128)(2,1)S(1)} %concatenate.29), channel_id=1, source_target_pairs={{0,16},{1,17},{2,18},{3,19},{4,20},{5,21},{6,22},{7,23},{8,24},{9,... | collective-permute-start | bytes 1179656 | tf_op jit(solution)/shard_map/ppermute | solution.py:59
  59.4 3.6 %copy-start.1 = (bf16[6,2048]{1,0:T(8,128)(2,1)S(1)}, bf16[6,2048]{1,0:T(8,128)(2,1)}, u32[]{:S(2)}) copy-start(bf16[6,2048]{1,0:T(8,128)(2,1)} %param.5) | copy-start | bytes 73732
  59.4 4.4 %copy-start.6 = (f32[7,80]{1,0:T(8,128)S(1)}, f32[7,80]{1,0:T(8,128)}, u32[]{:S(2)}) copy-start(f32[7,80]{1,0:T(8,128)} %constant.44) | copy-start | bytes 6724
  59.4 4.6 %copy-start.5 = (f32[7,80]{1,0:T(8,128)S(1)}, f32[7,80]{1,0:T(8,128)}, u32[]{:S(2)}) copy-start(f32[7,80]{1,0:T(8,128)} %constant.45) | copy-start | bytes 6724
  62.9 69.2 %copy-start.4 = (f32[7,80]{1,0:T(8,128)S(1)}, f32[7,80]{1,0:T(8,128)}, u32[]{:S(2)}) copy-start(f32[7,80]{1,0:T(8,128)} %constant.46) | copy-start | bytes 6724
  63.0 69.4 %copy-start.3 = (f32[7,80]{1,0:T(8,128)S(1)}, f32[7,80]{1,0:T(8,128)}, u32[]{:S(2)}) copy-start(f32[7,80]{1,0:T(8,128)} %constant.47) | copy-start | bytes 6724
  63.0 69.6 %copy-start.2 = (f32[16,80]{1,0:T(8,128)S(1)}, f32[16,80]{1,0:T(8,128)}, u32[]{:S(2)}) copy-start(f32[16,80]{1,0:T(8,128)} %constant.48) | copy-start | bytes 15364
  128.3 16.2 %all-to-all-start = ((f32[8,6,2,2048]{3,2,1,0:T(2,128)}), f32[8,6,2,2048]{3,2,1,0:T(2,128)S(1)}, u32[]{:S(2)}, u32[]{:S(2)}) async-start(f32[8,6,2,2048]{3,2,1,0:T(2,128)} %copy.11), calls=%async_computation.1 | async-start | bytes 1572864 | tf_op jit(solution)/shard_map/all_to_all | solution.py:82
Sparse Core Ops, SparseCore 0:
  63.1 62.5 reduce-scatter.1
